TPU v7x, 256 devices: a whole 4x4x8 slice. The times are simulated.
256 devices in a mesh: gx: 32 (over z, x), gy: 8 (over y, core).
Axes of the slice: x: 4, y: 4, z: 8, core: 2. Of those that a mesh axis runs over, the one named last changes fastest.
Arguments:
- orbitals: bfloat16 [20000, 200], P('gx'), may hold values from -6 to 6
- projector: bfloat16 [6016, 20000], P('gy', 'gx'), may hold values from -0.0390625 to 0.0390625
- integrals: bfloat16 [32, 6016, 6016], P('gx', 'gy'), may hold values from -1 to 1
Outputs:
- exchange_matrix: float32 [6016, 6016], P('gx', 'gy')
- exchange_orbitals: float32 [20000, 200], P('gx', 'gy')
- energy_mean: float32 [], replicated
- trace_mean: float32 [], replicated
All inputs are finite; a program needn't handle non-finite values.
Results may differ from a plain program's by a relative error of at most 0.008.
Values may be sent and summed in bfloat16 or wider, within the bound.
A program may use at most 128 MiB of HBM per device.

v0:
```python
import jax
import jax.numpy as jnp
from jax import lax
from jax.sharding import Mesh
from jax.sharding import PartitionSpec as P

GX = ("gx_0", "gx_1")
GY = ("gy_0", "gy_1")


def filled_up(lines, devices):
    spare = -lines.shape[0] % devices
    if not spare:
        return lines
    return jnp.concatenate([lines, jnp.zeros((spare, *lines.shape[1:]), lines.dtype)])


def from_everyone(shard, axis):
    copies = jnp.broadcast_to(shard, (lax.axis_size(axis), *shard.shape))
    return lax.all_to_all(copies, axis, split_axis=0, concat_axis=0, tiled=True)


def joined_along(parts, dim):
    parts = jnp.moveaxis(parts, 0, dim)
    lengths = parts.shape
    return parts.reshape(*lengths[:dim], lengths[dim] * lengths[dim + 1], *lengths[dim + 2 :])


def gather_directly(shard, axis, dim):
    parts = from_everyone(shard, axis)
    return joined_along(parts, dim)


def cut_along(shard, dim, devices):
    lengths = shard.shape
    parts = shard.reshape(*lengths[:dim], devices, lengths[dim] // devices, *lengths[dim + 1 :])
    return jnp.moveaxis(parts, dim, 0)


def sent_and_summed(shard, axis, dim):
    devices = lax.axis_size(axis)
    parts = lax.all_to_all(cut_along(shard, dim, devices), axis, 0, 0, tiled=True)
    return jnp.sum(parts, axis=0)


def nested_sum(shard, axes):
    lines = shard.reshape(-1)
    padded = filled_up(lines, lax.axis_size(axes))
    whole = gather_directly(sent_and_summed(padded, axes, 0), axes, 0)
    return lax.slice_in_dim(whole, 0, len(lines)).reshape(shard.shape)


def whole_of(shard, axes, dim):
    far, near = axes
    initial = from_everyone(shard, far)
    parts = jnp.swapaxes(from_everyone(initial, near), 0, 1)
    return joined_along(parts.reshape(-1, *shard.shape), dim)


def from_root(shard, axes, root):
    shard = jnp.where(lax.axis_index(axes) == root, shard, jnp.zeros_like(shard))
    for axis in axes:
        shard = lax.psum(shard, axis)
    return shard


def of_everyone(shard, axis):
    everything = from_everyone(shard, axis)
    return jnp.sum(everything, axis=0)


def over_axes(shard, axes):
    far, near = axes
    return of_everyone(of_everyone(shard, near), far)


def packed_total(arrays, axis):
    ends = [0]
    for a in arrays:
        ends.append(ends[-1] + a.size)
    subtotal = over_axes(jnp.concatenate([a.ravel() for a in arrays]), axis)
    return tuple((subtotal[b:e].reshape(a.shape) for a, b, e in zip(arrays, ends, ends[1:])))


def sent_and_summed_2(shard, axis, dim):
    devices = lax.axis_size(axis)
    parts = lax.all_to_all(cut_along(shard, dim, devices), axis, 0, 0, tiled=True)
    return jnp.sum(parts.astype(jnp.float32), axis=0)


def on_device(orbitals, projector, integrals):
    part_rows = projector.shape[0]
    partial_value = jnp.dot(projector, orbitals, preferred_element_type=jnp.float32)
    own_admm = nested_sum(partial_value, GX).astype(jnp.bfloat16)
    admm = whole_of(own_admm, ("gy_0", "gy_1"), 0)
    half = lax.dot_general(
        integrals, admm, (((2,), (0,)), ((), ())), preferred_element_type=jnp.float32
    ).astype(jnp.bfloat16)
    size_x = lax.axis_size(GX)
    block_rows = admm.shape[0] // size_x
    index_x = lax.axis_index(GX)
    index_y = lax.axis_index(GY)
    all_half = lax.all_gather(half, GX, axis=0, tiled=True)
    first_row = index_x * block_rows
    root = first_row // part_rows
    offset = jnp.clip(first_row - index_y * part_rows, 0, part_rows - block_rows)
    mine = lax.dynamic_slice_in_dim(all_half, offset, block_rows, 1)
    columns = from_root(mine, GY, root)
    exchange = lax.dot_general(
        columns, all_half, (((0, 2), (0, 2)), ((), ())), preferred_element_type=jnp.float32
    )
    row_ids = index_x * block_rows + lax.iota(jnp.int32, block_rows)
    col_ids = index_y * part_rows + lax.iota(jnp.int32, part_rows)
    diag_mask = row_ids[:, None] == col_ids[None, :]
    trace_part = jnp.sum(jnp.where(diag_mask, exchange, 0.0))
    admm_wide = admm.astype(jnp.float32)
    col_orbs = lax.dynamic_slice_in_dim(admm_wide, index_x * block_rows, block_rows, 0)
    row_orbs = lax.dynamic_slice_in_dim(admm_wide, index_y * part_rows, part_rows, 0)
    applied_part = lax.dot_general(
        exchange,
        col_orbs,
        (((0,), (0,)), ((), ())),
        precision=lax.Precision.HIGHEST,
        preferred_element_type=jnp.float32,
    )
    energy_part = jnp.sum(row_orbs * applied_part)
    energy_total, trace_total = packed_total(
        (energy_part, trace_part), (("gx_0", "gx_1"), ("gy_0", "gy_1"))
    )
    applied = nested_sum(applied_part, GX)
    applied_low = applied.astype(jnp.bfloat16)
    back_part = lax.dot_general(
        projector, applied_low, (((0,), (0,)), ((), ())), preferred_element_type=jnp.float32
    )
    back = sent_and_summed_2(back_part.astype(jnp.bfloat16), GY, 1)
    total_adm = admm.shape[0]
    energy_mean = -0.5 * energy_total / (total_adm * admm.shape[1])
    trace_mean = trace_total / total_adm
    return (exchange, back, energy_mean, trace_mean)


def solution(mesh):
    finer = Mesh(mesh.devices.reshape(8, 4, 4, 2), ("gx_0", "gx_1", "gy_0", "gy_1"))
    return jax.shard_map(
        on_device,
        mesh=finer,
        in_specs=(P(GX, None), P(GY, GX), P(GX, GY, None)),
        out_specs=(P(GX, GY), P(GX, GY), P(), P()),
        check_vma=False,
    )
```

profile of v0, /device:TPU:9, one launch (start us, length us, event | category | flops | bytes accessed | tf_op | source)
XLA Modules:
  0.0 443.9 jit_solution(7232051091509492332)
XLA Ops:
  11.0 28.7 %all_to_all.59 = f32[32,1,4700]{2,1,0:T(1,128)S(1)} all-to-all(f32[32,1,4700]{2,1,0:T(1,128)S(1)} %all_to_all.48), channel_id=1, replica_groups=mesh['gx_0'=8,'gx_1'=4,'gy_0'=4,'gy_1'=2] {'gx_0','gx_1'}, dimensions={0} | all-to-all | bytes 1203200 | tf_op jit(solution)/shard_map/all_to_all | solution.py:42
  41.1 2.6 reduce.8
  44.0 16.2 %all_to_all.60 = bf16[32,2,2350]{2,1,0:T(2,128)(2,1)S(1)} all-to-all(bf16[32,2,2350]{2,1,0:T(2,128)(2,1)S(1)} %reshape.74), channel_id=1, replica_groups=mesh['gx_0'=8,'gx_1'=4,'gy_0'=4,'gy_1'=2] {'gx_0','gx_1'}, dimensions={0} | all-to-all | bytes 601600 | tf_op jit(solution)/shard_map/all_to_all | solution.py:20
  63.1 15.9 %all_to_all.61 = bf16[4,752,200]{1,2,0:T(8,128)(2,1)S(1)} all-to-all(bf16[4,752,200]{1,2,0:T(8,128)(2,1)S(1)} %broadcast_in_dim.28), channel_id=1, replica_groups=mesh['gx_0'=8,'gx_1'=4,'gy_0'=4,'gy_1'=2] {'gy_0'}, dimensions={0} | all-to-all | bytes 2406400 | tf_op jit(solution)/shard_map/all_to_all | solution.py:20
  80.2 10.4 %all_to_all.62 = bf16[2,4,752,200]{2,1,3,0:T(4,128)(2,1)S(1)} all-to-all(bf16[2,4,752,200]{2,1,3,0:T(4,128)(2,1)S(1)} %broadcast_in_dim.29), channel_id=1, replica_groups=mesh['gx_0'=8,'gx_1'=4,'gy_0'=4,'gy_1'=2] {'gy_1'}, dimensions={0} | all-to-all | bytes 4812800 | tf_op jit(solution)/shard_map/all_to_all | solution.py:20
  90.6 3.8 copy.32
  94.4 4.6 %reshape_reshape.2 = bf16[6016,200]{0,1:T(8,128)(2,1)} reshape(bf16[4,2,752,200]{2,1,0,3:T(2,128)(2,1)S(1)} %copy.32) | data formatting | bytes 4812800 | tf_op jit(solution)/shard_map/reshape;reshape | solution.py:26
  99.0 7.8 %fusion.5 = bf16[1,752,200]{1,2,0:T(8,128)(2,1)} fusion(bf16[6016,200]{0,1:T(8,128)(2,1)} %reshape_reshape.2, bf16[1,752,6016]{2,1,0:T(8,128)(2,1)} %param.5), kind=kOutput, calls=%fused_computation.6 | convolution fusion | flops 1809763200 | bytes 11755264 | tf_op jit(solution)/shard_map/dot_general | solution.py:96
  106.9 100.5 %all-gather.4.cloned.1.call-done = bf16[32,752,200]{1,2,0:T(8,128)(2,1)} async-done(((bf16[1,752,200]{1,2,0:T(8,128)(2,1)}), bf16[32,752,200]{1,2,0:T(8,128)(2,1)}) %all-gather.4.cloned.1.call-update) | async-done | bytes 9625616 | tf_op jit(solution)/shard_map/all_gather | solution.py:103
  207.5 5.8 %constant_dynamic-slice_fusion = bf16[32,188,200]{1,2,0:T(8,128)(2,1)} fusion(bf16[32,752,200]{1,2,0:T(8,128)(2,1)} %all-gather.4.cloned.1.call-done, s32[]{:T(128)S(6)} %min.4), kind=kLoop, calls=%fused_computation.18 | loop fusion | bytes 4812804 | tf_op jit(solution)/shard_map/dynamic_slice | solution.py:107
  213.3 5.7 %copy.41 = bf16[32,188,200]{2,1,0:T(8,128)(2,1)} copy(bf16[32,188,200]{1,2,0:T(8,128)(2,1)} %constant_dynamic-slice_fusion) | data formatting | bytes 4812800
  221.1 79.1 %all-reduce.3.cloned.1.call-done = bf16[32,188,200]{2,1,0:T(8,128)(2,1)} async-done(((bf16[32,188,200]{2,1,0:T(8,128)(2,1)}), bf16[32,188,200]{2,1,0:T(8,128)(2,1)}) %all-reduce.3.cloned.1.call-update) | async-done | bytes 2406416 | tf_op jit(solution)/shard_map/psum | solution.py:63
  300.3 38.3 %all-reduce.5.cloned.1.call-done = bf16[32,188,200]{2,1,0:T(8,128)(2,1)} async-done(((bf16[32,188,200]{2,1,0:T(8,128)(2,1)}), bf16[32,188,200]{2,1,0:T(8,128)(2,1)}) %all-reduce.5.cloned.1.call-update) | async-done | bytes 2406416 | tf_op jit(solution)/shard_map/psum | solution.py:63
  338.6 7.7 %select_reduce_fusion = (f32[]{:T(128)}, f32[188,752]{1,0:T(8,128)S(1)}) fusion(s32[752]{0:T(1024)S(1)} %iota_add_fusion, s32[188]{0:T(256)S(1)} %iota_add_fusion.1, bf16[32,188,200]{2,1,0:T(8,128)(2,1)} %all-reduce.5.cloned.1.call-done, bf16[32,752,200]{1,2,0:T(8,128)(2,1)} %all-gather.4.cloned.1.call-done), kind=kOutput, calls=%fused_computation.12 | convolution fusion | flops 1810036736 | bytes 12601268 | tf_op jit(solution)/shard_map/dot_general | solution.py:109
  351.0 9.5 %all-to-all-start.4 = ((f32[32,1,4700]{2,1,0:T(1,128)}), f32[32,1,4700]{2,1,0:T(1,128)S(1)}, u32[]{:S(2)}, u32[]{:S(2)}) async-start(f32[32,1,4700]{2,1,0:T(1,128)} %all_to_all.49), calls=%async_computation.4 | async-start | bytes 1212416 | tf_op jit(solution)/shard_map/all_to_all | solution.py:42
  361.9 16.7 %all-to-all-done.4 = f32[32,1,4700]{2,1,0:T(1,128)S(1)} async-done(((f32[32,1,4700]{2,1,0:T(1,128)}), f32[32,1,4700]{2,1,0:T(1,128)S(1)}, u32[]{:S(2)}, u32[]{:S(2)}) %all-to-all-start.4) | async-done | bytes 601632 | tf_op jit(solution)/shard_map/all_to_all | solution.py:42
  379.2 6.6 %all-to-all-start.7 = ((f32[8,1,2]{2,1,0:T(1,128)}), f32[8,1,2]{2,1,0:T(1,128)S(1)}, u32[]{:S(2)}, u32[]{:S(2)}) async-start(f32[8,1,2]{2,1,0:T(1,128)} %broadcast_in_dim.33), calls=%async_computation.7 | async-start | bytes 8192 | tf_op jit(solution)/shard_map/all_to_all | solution.py:20
  386.6 2.6 reduce.9
  390.3 4.6 %all-to-all-start.5 = ((bf16[32,2,2350]{2,1,0:T(2,128)(2,1)}), bf16[32,2,2350]{2,1,0:T(2,128)(2,1)S(1)}, u32[]{:S(2)}, u32[]{:S(2)}) async-start(bf16[32,2,2350]{2,1,0:T(2,128)(2,1)} %reshape.76), calls=%async_computation.5 | async-start | bytes 622592 | tf_op jit(solution)/shard_map/all_to_all | solution.py:20
  394.9 12.5 %all-to-all-done.5 = bf16[32,2,2350]{2,1,0:T(2,128)(2,1)S(1)} async-done(((bf16[32,2,2350]{2,1,0:T(2,128)(2,1)}), bf16[32,2,2350]{2,1,0:T(2,128)(2,1)S(1)}, u32[]{:S(2)}, u32[]{:S(2)}) %all-to-all-start.5) | async-done | bytes 300832 | tf_op jit(solution)/shard_map/all_to_all | solution.py:20
  408.0 4.7 %all-to-all-start.8 = ((f32[32,1,2]{2,1,0:T(1,128)}), f32[32,1,2]{2,1,0:T(1,128)S(1)}, u32[]{:S(2)}, u32[]{:S(2)}) async-start(f32[32,1,2]{2,1,0:T(1,128)} %broadcast_in_dim.34), calls=%async_computation.8 | async-start | bytes 32768 | tf_op jit(solution)/shard_map/all_to_all | solution.py:20
  416.6 4.6 %all-to-all-done.8 = f32[32,1,2]{2,1,0:T(1,128)S(1)} async-done(((f32[32,1,2]{2,1,0:T(1,128)}), f32[32,1,2]{2,1,0:T(1,128)S(1)}, u32[]{:S(2)}, u32[]{:S(2)}) %all-to-all-start.8) | async-done | bytes 288 | tf_op jit(solution)/shard_map/all_to_all | solution.py:20
  421.2 7.2 %all-to-all-start.6 = ((bf16[8,625,25]{1,2,0:T(8,128)(2,1)}), bf16[8,625,25]{1,2,0:T(8,128)(2,1)S(1)}, u32[]{:S(2)}, u32[]{:S(2)}) async-start(bf16[8,625,25]{1,2,0:T(8,128)(2,1)} %bitcast.6), calls=%async_computation.6 | async-start | bytes 655360 | tf_op jit(solution)/shard_map/all_to_all | solution.py:87
  430.3 4.1 all-to-all-done.6
  (45 shorter events, 26.1 us)
Async XLA Ops:
  7.2 1.2 copy-start
  7.2 200.3 %all-gather.4.cloned.1.call-start = ((), (), s32[]{:S(2)}) async-start(), calls=%async_computation.11 | async-start | bytes 10137600 | tf_op jit(solution)/shard_map/all_gather | solution.py:103
  106.9 193.4 %all-reduce.3.cloned.1.call-start = ((), (), s32[]{:S(2)}) async-start(), calls=%async_computation.9 | async-start | bytes 6291456 | tf_op jit(solution)/shard_map/psum | solution.py:63
  220.8 117.8 %all-reduce.5.cloned.1.call-start = ((), (), s32[]{:S(2)}) async-start(), calls=%async_computation.10 | async-start | bytes 6291456 | tf_op jit(solution)/shard_map/psum | solution.py:63
  346.3 40.3 %copy-start.1 = (f32[188,752]{1,0:T(8,128)}, f32[188,752]{1,0:T(8,128)S(1)}, u32[]{:S(2)}) copy-start(f32[188,752]{1,0:T(8,128)S(1)} %get-tuple-element.7) | copy-start | bytes 1696516
  351.0 27.6 %all-to-all-start.4 = ((f32[32,1,4700]{2,1,0:T(1,128)}), f32[32,1,4700]{2,1,0:T(1,128)S(1)}, u32[]{:S(2)}, u32[]{:S(2)}) async-start(f32[32,1,4700]{2,1,0:T(1,128)} %all_to_all.49), calls=%async_computation.4 | async-start | bytes 1212416 | tf_op jit(solution)/shard_map/all_to_all | solution.py:42
  379.2 11.1 %all-to-all-start.7 = ((f32[8,1,2]{2,1,0:T(1,128)}), f32[8,1,2]{2,1,0:T(1,128)S(1)}, u32[]{:S(2)}, u32[]{:S(2)}) async-start(f32[8,1,2]{2,1,0:T(1,128)} %broadcast_in_dim.33), calls=%async_computation.7 | async-start | bytes 8192 | tf_op jit(solution)/shard_map/all_to_all | solution.py:20
  390.3 17.1 %all-to-all-start.5 = ((bf16[32,2,2350]{2,1,0:T(2,128)(2,1)}), bf16[32,2,2350]{2,1,0:T(2,128)(2,1)S(1)}, u32[]{:S(2)}, u32[]{:S(2)}) async-start(bf16[32,2,2350]{2,1,0:T(2,128)(2,1)} %reshape.76), calls=%async_computation.5 | async-start | bytes 622592 | tf_op jit(solution)/shard_map/all_to_all | solution.py:20
  408.0 13.2 %all-to-all-start.8 = ((f32[32,1,2]{2,1,0:T(1,128)}), f32[32,1,2]{2,1,0:T(1,128)S(1)}, u32[]{:S(2)}, u32[]{:S(2)}) async-start(f32[32,1,2]{2,1,0:T(1,128)} %broadcast_in_dim.34), calls=%async_computation.8 | async-start | bytes 32768 | tf_op jit(solution)/shard_map/all_to_all | solution.py:20
  421.2 13.2 %all-to-all-start.6 = ((bf16[8,625,25]{1,2,0:T(8,128)(2,1)}), bf16[8,625,25]{1,2,0:T(8,128)(2,1)S(1)}, u32[]{:S(2)}, u32[]{:S(2)}) async-start(bf16[8,625,25]{1,2,0:T(8,128)(2,1)} %bitcast.6), calls=%async_computation.6 | async-start | bytes 655360 | tf_op jit(solution)/shard_map/all_to_all | solution.py:87
Sparse Core Ops, SparseCore 0:
  107.0 100.4 all-gather.3
  221.0 79.2 all-reduce.2
  302.8 35.7 all-reduce.4
where the time goes:
time: 447 us; the launch traced here: 444 us
  waiting for transfers between devices  256 us (57%)
  blocking collectives  71.2 us (16%)
  local copies, waits for them, and re-layouts  36.3 us (8%)
  starting transfers between devices  32.9 us (7%)
  matrix products  19.8 us (4%)
  between operations  17.5 us (4%)
  other arithmetic  10.2 us (2%)
    psum x2, waiting for transfers between devices, from_root(): shard = lax.psum(shard, axis)  117 us
    all_gather x1, waiting for transfers between devices, on_device(): all_half = lax.all_gather(half, GX, axis=0, tiled=True)  101 us
    all_to_all x3, blocking collectives, from_everyone(): return lax.all_to_all(copies, axis, split_axis=0, concat_axis=0, tiled=True)  42.5 us
    all_to_all x1, blocking collectives, sent_and_summed(): lax.all_to_all(cut_along(shard, dim, devices), axis, 0, 0, tiled=True)  28.7 us
    all_to_all x3, waiting for transfers between devices, from_everyone(): return lax.all_to_all(copies, axis, split_axis=0, concat_axis=0, tiled=True)  17.1 us
    all_to_all x1, waiting for transfers between devices, sent_and_summed(): lax.all_to_all(cut_along(shard, dim, devices), axis, 0, 0, tiled=True)  16.7 us
    all_to_all x3, starting transfers between devices, from_everyone(): return lax.all_to_all(copies, axis, split_axis=0, concat_axis=0, tiled=True)  15.9 us
    all_to_all x1, starting transfers between devices, sent_and_summed(): lax.all_to_all(cut_along(shard, dim, devices), axis, 0, 0, tiled=True)  9.54 us
  transfers between devices with their start and end apart: 8, of which 7 were waited for; matrix products, arithmetic and copies ran while one was open for 2% of the time, Pallas kernels for 0%

commit v1 on v0

v1 whole, which is shorter than its diff:
```python
import functools

import jax
import jax.numpy as jnp
from jax import lax
from jax.experimental import pallas as pl
from jax.experimental.pallas import tpu as pltpu
from jax.sharding import PartitionSpec as P

MESH = pl.DeviceIdType.MESH
F32, BF16 = jnp.float32, jnp.bfloat16
NZ, NX, NY, NC = 8, 4, 4, 2
NG = NY * NC
PIECES = 6


def dot(a, b, ca, cb):
    return lax.dot_general(a, b, (((ca,), (cb,)), ((), ())), preferred_element_type=F32)


class Links:
    def __init__(self, send_sems, recv_sems, partner):
        self.send_sems, self.recv_sems, self.partner = send_sems, recv_sems, partner
        self.n_send = self.n_recv = 0
        self.pending = []

    def slot(self):
        self.n_recv += 1
        return self.n_recv - 1

    def send(self, src, dst, device, slot, pred=None):
        copy = pltpu.make_async_remote_copy(
            src_ref=src,
            dst_ref=dst,
            send_sem=self.send_sems.at[self.n_send],
            recv_sem=self.recv_sems.at[slot],
            device_id=device,
            device_id_type=MESH,
        )
        self.n_send += 1
        self.pending.append((copy, pred))
        if pred is None:
            copy.start()
        else:
            pl.when(pred)(copy.start)

    def arrived(self, dst, slot, pred=None):
        copy = pltpu.make_async_remote_copy(
            src_ref=dst,
            dst_ref=dst,
            send_sem=self.send_sems.at[0],
            recv_sem=self.recv_sems.at[slot],
            device_id=self.partner,
            device_id_type=MESH,
        )
        if pred is None:
            copy.wait_recv()
        else:
            pl.when(pred)(copy.wait_recv)

    def drain(self):
        for copy, pred in self.pending:
            if pred is None:
                copy.wait_send()
            else:
                pl.when(pred)(copy.wait_send)
        self.pending = []


def interleave(*flows):
    flows = list(flows)
    while flows:
        for flow in list(flows):
            try:
                next(flow)
            except StopIteration:
                flows.remove(flow)


def kernel(
    orb_ref,
    proj_ref,
    int_ref,
    exch_ref,
    back_ref,
    scal_ref,
    iv,
    pp,
    part,
    xs,
    xr,
    zs,
    zr,
    stage,
    full,
    hf,
    h16,
    hp,
    hh,
    acc,
    psend,
    prcv,
    ts,
    tr,
    tfull,
    dxs,
    dxr,
    dzs,
    dzr,
    ap,
    bk,
    bkr,
    sc,
    sr1,
    sr2,
    sr3,
    send_sems,
    recv_sems,
    int_sem,
):
    gx, gy = lax.axis_index("gx"), lax.axis_index("gy")
    z, x = gx // NX, gx % NX
    y, c = gy // NC, gy % NC
    rows = proj_ref.shape[0]
    npri = proj_ref.shape[1]
    nocc = orb_ref.shape[1]
    out_rows = rows // NX

    load = pltpu.make_async_copy(int_ref.at[0], iv, int_sem)
    load.start()

    def at(dz=0, dx=0, dy=0, dg=0):
        zz, xx = (z + dz) % NZ, (x + dx) % NX
        if dg:
            gg = (gy + dg) % NG
        else:
            gg = ((y + dy) % NY) * NC + c
        return (zz * NX + xx, gg)

    partner = (gx, y * NC + (1 - c))
    links = Links(send_sems, recv_sems, partner)

    barrier = pltpu.get_barrier_semaphore()
    peers = [at(dz=d) for d in range(1, NZ)] + [at(dx=d) for d in range(1, NX)]
    peers += [at(dg=d) for d in range(1, NG)]
    for peer in peers:
        pl.semaphore_signal(barrier, inc=1, device_id=peer, device_id_type=MESH)

    pp[...] = jnp.zeros_like(pp)
    pp[0:rows, 0:npri] = proj_ref[...]
    part[...] = jnp.zeros_like(part)
    part[0:rows, 0:nocc] = dot(proj_ref[...], orb_ref[...], 1, 0)
    hf[...] = jnp.zeros_like(hf)
    hp[...] = jnp.zeros_like(hp)
    bk[...] = jnp.zeros_like(bk)
    pl.semaphore_wait(barrier, len(peers))

    def ring4(dim, whole, halves, on_arrival=None):
        me = {"x": x, "y": y}[dim]
        step = (lambda d: at(dx=d)) if dim == "x" else (lambda d: at(dy=d))
        a, b, o0, o1 = links.slot(), links.slot(), links.slot(), links.slot()
        left, right, far = (me + 3) % 4, (me + 1) % 4, (me + 2) % 4
        links.send(whole(me), whole(me), step(1), a)
        links.send(whole(me), whole(me), step(3), b)
        yield
        links.arrived(whole(left), a)
        links.send(halves(left, 0), halves(left, 0), step(1), o0)
        if on_arrival:
            on_arrival(whole, left)
        yield
        links.arrived(whole(right), b)
        links.send(halves(right, 1), halves(right, 1), step(3), o1)
        if on_arrival:
            on_arrival(whole, right)
        yield
        links.arrived(halves(far, 0), o0)
        links.arrived(halves(far, 1), o1)
        if on_arrival:
            on_arrival(whole, far)

    def reduce_xz(src_ref, xs, xr, zs, zr, piece):
        xs[...] = src_ref[...].astype(BF16)
        slots = [links.slot() for _ in range(1, NX)]
        for d in range(1, NX):
            to = (x + d) % NX
            links.send(xs.at[pl.ds(to * 192, 192), :], xr.at[d - 1], at(dx=d), slots[d - 1])
        yield
        total = src_ref[pl.ds(x * 192, 192), :]
        for d in range(1, NX):
            links.arrived(xr.at[d - 1], slots[d - 1])
            total = total + xr[d - 1].astype(F32)
        src_ref[pl.ds(x * 192, 192), :] = total
        zs[...] = total.astype(BF16)
        slots = [links.slot() for _ in range(1, NZ)]
        for d in range(1, NZ):
            to = (z + d) % NZ
            first = jnp.minimum(to, PIECES - 1) * 32
            links.send(zs.at[pl.ds(first, 32), :], zr.at[d - 1], at(dz=d), slots[d - 1], to < PIECES)
        yield
        owner = z < PIECES
        for d in range(1, NZ):
            links.arrived(zr.at[d - 1], slots[d - 1], owner)

        own = jnp.minimum(z, PIECES - 1)

        @pl.when(owner)
        def _():
            total = src_ref[pl.ds(x * 192 + own * 32, 32), :]
            for d in range(1, NZ):
                total = total + zr[d - 1].astype(F32)
            piece(x, own)[...] = total.astype(BF16)

        slots = [links.slot() for _ in range(1, NZ)]
        for d in range(1, NZ):
            links.send(piece(x, own), piece(x, own), at(dz=d), slots[d - 1], owner)
        yield
        for d in range(1, NZ):
            src = (z + NZ - d) % NZ
            links.arrived(piece(x, jnp.minimum(src, PIECES - 1)), slots[d - 1], src < PIECES)

    def to_partner_y(blocks):
        def go(whole, i):
            slot = links.slot()
            links.send(whole(i), whole(i), partner, slot)
            core_waits.append((blocks, i, slot))

        return go

    core_waits = []
    interleave(
        reduce_xz(part, xs, xr, zs, zr, lambda i, k: stage.at[y, c, i, pl.ds(k * 32, 32), :])
    )
    interleave(
        ring4("x", lambda i: stage.at[y, c, i, 0:96, :], lambda i, h: stage.at[y, c, i, 48 * h : 48 * h + 48, :]),
        ring4("y", lambda i: stage.at[i, c, x, 96:192, :], lambda i, h: stage.at[i, c, x, 96 + 48 * h : 144 + 48 * h, :]),
    )
    low = lambda i: stage.at[i, c, :, 0:96, :]
    high = lambda i: stage.at[:, c, i, 96:192, :]
    low_other = lambda i: stage.at[i, 1 - c, :, 0:96, :]
    high_other = lambda i: stage.at[:, 1 - c, i, 96:192, :]
    to_partner_y(low_other)(low, y)
    to_partner_y(high_other)(high, x)
    interleave(
        ring4("y", low, lambda i, h: stage.at[i, c, 2 * h : 2 * h + 2, 0:96, :], to_partner_y(low_other)),
        ring4("x", high, lambda i, h: stage.at[2 * h : 2 * h + 2, c, i, 96:192, :], to_partner_y(high_other)),
    )
    for other, i, slot in core_waits:
        links.arrived(other(i), slot)
    for a in range(NY):
        for b in range(NC):
            for k in range(NX):
                n = min(192, rows - 192 * k)
                r0 = rows * (a * NC + b) + 192 * k
                full[r0 : r0 + n, :] = stage[a, b, k, 0:n, :]

    load.wait()
    for r0 in range(0, rows, 256):
        n = min(256, rows - r0)
        hf[r0 : r0 + n, :] = dot(iv[r0 : r0 + n, :], full[...], 1, 0)
    h16[...] = hf[...].astype(BF16)
    hr = h16[...].astype(F32)
    trace = jnp.sum(hr * hr)
    for k in range(NX):
        hp[192 * k : 192 * k + out_rows, :] = hf[out_rows * k : out_rows * (k + 1), :]
    hh[0, 0] = jnp.transpose(hp[...])[0:208, :].astype(BF16)

    ys, cs = z // NC, z % NC
    dy = (y + NY - ys) % NY
    on = c == cs
    is_src = on & (dy == 0)
    not_src = jnp.logical_not(is_src)
    is_next, is_prev = on & (dy == 1), on & (dy == 3)
    relay = on & (dy != 0)
    lhs_at = jnp.where(is_src, 0, 1)
    up, down, yup, ydown = at(dz=1), at(dz=NZ - 1), at(dy=1), at(dy=NY - 1)

    def half_of(which, s, h):
        return hh.at[which, s, :, 384 * h : 384 * h + 384]

    def flow_exchange():
        col_slots = {(s, h): links.slot() for s in range(1, NZ) for h in range(2)}
        row_slots = {(s, h): links.slot() for s in range(NZ) for h in range(2)}

        def spread(s, h):
            src, dst = half_of(0, s, h), half_of(1, s, h)
            for device in (yup, ydown, partner):
                links.send(src, dst, device, row_slots[s, h], is_src)

        def rows_in(s):
            for h in range(2):
                blk = half_of(1, s, h)
                links.arrived(blk, row_slots[s, h], not_src)
                if h == 0:
                    links.send(blk, blk, yup, row_slots[s, h], is_next)
                else:
                    links.send(blk, blk, ydown, row_slots[s, h], is_prev)
                links.send(blk, blk, partner, row_slots[s, h], relay)

        def accumulate(s, first=False):
            @pl.loop(0, 6)
            def _(m):
                cols = pl.ds(pl.multiple_of(m * 128, 128), 128)
                value = dot(hh[lhs_at, s, :, cols], hh[0, s], 0, 0)
                if first:
                    acc[cols, :] = value
                else:
                    acc[cols, :] += value

        for h in range(2):
            links.send(half_of(0, 0, h), half_of(0, 1, h), up, col_slots[1, h])
            links.send(half_of(0, 0, 1 - h), half_of(0, 7, 1 - h), down, col_slots[7, 1 - h])
        for h in range(2):
            spread(0, h)
        yield
        ready = [0]
        for k in (1, 2, 3):
            for j in range(2):
                h = j
                links.arrived(half_of(0, k, h), col_slots[k, h])
                if k < 3 or h == 0:
                    links.send(half_of(0, k, h), half_of(0, k + 1, h), up, col_slots[k + 1, h])
                spread(k, h)
                h = 1 - j
                links.arrived(half_of(0, 8 - k, h), col_slots[8 - k, h])
                if k < 3 or h == 1:
                    links.send(half_of(0, 8 - k, h), half_of(0, 7 - k, h), down, col_slots[7 - k, h])
                spread(8 - k, h)
            yield
            for s in ready:
                rows_in(s)
                accumulate(s, s == 0)
            ready = [k, 8 - k]
            yield
        for h in range(2):
            links.arrived(half_of(0, 4, h), col_slots[4, h])
            spread(4, h)
        yield
        for s in ready + [4]:
            rows_in(s)
            accumulate(s)
        slots = [links.slot() for _ in range(1, NX)]
        psend[...] = acc[...].astype(BF16)
        for d in range(1, NX):
            to = (x + d) % NX
            links.send(psend.at[pl.ds(to * 192, 192), :], prcv.at[d - 1], at(dx=d), slots[d - 1])
        yield
        total = acc[pl.ds(x * 192, 192), :]
        for d in range(1, NX):
            links.arrived(prcv.at[d - 1], slots[d - 1])
            total = total + prcv[d - 1].astype(F32)
        lane = lax.broadcasted_iota(jnp.int32, total.shape, 1)
        out = total
        for k in range(1, NX):
            moved = pltpu.roll(total, total.shape[1] - 4 * k, 1)
            out = jnp.where(lane >= out_rows * k, moved, out)
        exch_ref[...] = out[0:out_rows, 0:rows]

    def flow_applied():
        own = stage[y, c].reshape(4 * 192, 256)
        tt = dot(own, h16[...], 0, 0).astype(BF16)
        share = nocc // NG
        r = lax.broadcasted_iota(jnp.int32, (256, 256), 0)
        j = lax.broadcasted_iota(jnp.int32, (256, 256), 1)
        pick = ((r % 32 < share) & (j == share * (r // 32) + r % 32)).astype(F32).astype(BF16)
        ts[...] = dot(pick, tt, 1, 0).astype(BF16)
        slots = [links.slot() for _ in range(1, NG)]
        for d in range(1, NG):
            to = (gy + d) % NG
            links.send(ts.at[pl.ds(to * 32, 32), :], tr.at[d - 1], at(dg=d), slots[d - 1])
        yield
        total = ts[pl.ds(gy * 32, 32), :].astype(F32)
        for d in range(1, NG):
            links.arrived(tr.at[d - 1], slots[d - 1])
            total = total + tr[d - 1].astype(F32)
        energy = jnp.sum(total * total)
        tfull[pl.ds(gy * 32, 32), :] = total.astype(BF16)
        slots = [links.slot() for _ in range(1, NG)]
        s1 = [links.slot() for _ in range(1, NG)]
        mine = tfull.at[pl.ds(gy * 32, 32), :]
        sc[0] = jnp.where(lax.broadcasted_iota(jnp.int32, (8, 128), 0) == 0, trace, energy)
        for d in range(1, NG):
            links.send(mine, mine, at(dg=d), slots[d - 1])
            links.send(sc.at[0], sr1.at[d - 1], at(dg=d), s1[d - 1])
        yield
        for d in range(1, NG):
            src = (gy + NG - d) % NG
            links.arrived(tfull.at[pl.ds(src * 32, 32), :], slots[d - 1])
        part[...] = dot(h16[...], tfull[...], 1, 1)
        total = sc[0]
        for d in range(1, NG):
            links.arrived(sr1.at[d - 1], s1[d - 1])
            total = total + sr1[d - 1]
        sc[1] = total
        s2 = [links.slot() for _ in range(1, NX)]
        for d in range(1, NX):
            links.send(sc.at[1], sr2.at[d - 1], at(dx=d), s2[d - 1])
        for _ in reduce_xz(part, dxs, dxr, dzs, dzr, lambda i, k: ap.at[i, pl.ds(k * 32, 32), :]):
            yield
        total = sc[1]
        for d in range(1, NX):
            links.arrived(sr2.at[d - 1], s2[d - 1])
            total = total + sr2[d - 1]
        sc[2] = total
        s3 = [links.slot() for _ in range(1, NZ)]
        for d in range(1, NZ):
            links.send(sc.at[2], sr3.at[d - 1], at(dz=d), s3[d - 1])
        for _ in ring4("x", lambda i: ap.at[i], lambda i, h: ap.at[i, 96 * h : 96 * h + 96, :]):
            yield
        bt = dot(ap[...].reshape(4 * 192, 256), pp[...], 0, 0)
        bk[...] = bt.astype(BF16)
        slots = [links.slot() for _ in range(1, NG)]
        for d in range(1, NG):
            to = (gy + d) % NG
            links.send(bk.at[pl.ds(to * 32, 32), :], bkr.at[d - 1], at(dg=d), slots[d - 1])
        yield
        total = bk[pl.ds(gy * 32, 32), :].astype(F32)
        for d in range(1, NG):
            links.arrived(bkr.at[d - 1], slots[d - 1])
            total = total + bkr[d - 1].astype(F32)
        back_ref[...] = total
        total = sc[2]
        for d in range(1, NZ):
            links.arrived(sr3.at[d - 1], s3[d - 1])
            total = total + sr3[d - 1]
        scal_ref[...] = total

    interleave(flow_exchange(), flow_applied())
    links.drain()


N_SEMS = 320


def on_device(orbitals, projector, integrals):
    rows, npri = projector.shape
    total_adm = integrals.shape[2]
    nocc = orbitals.shape[1]
    out_rows = rows // NX
    vmem = pl.BlockSpec(memory_space=pltpu.VMEM)
    scratch = [
        pltpu.VMEM((rows, total_adm), BF16),
        pltpu.VMEM((768, 640), BF16),
        pltpu.VMEM((768, 256), F32),
        pltpu.VMEM((768, 256), BF16),
        pltpu.VMEM((3, 192, 256), BF16),
        pltpu.VMEM((192, 256), BF16),
        pltpu.VMEM((7, 32, 256), BF16),
        pltpu.VMEM((NY, NC, NX, 192, 256), BF16),
        pltpu.VMEM((total_adm, 256), BF16),
        pltpu.VMEM((768, 256), F32),
        pltpu.VMEM((768, 256), BF16),
        pltpu.VMEM((768, 256), F32),
        pltpu.VMEM((2, NZ, 208, 768), BF16),
        pltpu.VMEM((768, 768), F32),
        pltpu.VMEM((768, 768), BF16),
        pltpu.VMEM((3, 192, 768), BF16),
        pltpu.VMEM((256, 256), BF16),
        pltpu.VMEM((7, 32, 256), BF16),
        pltpu.VMEM((256, 256), BF16),
        pltpu.VMEM((768, 256), BF16),
        pltpu.VMEM((3, 192, 256), BF16),
        pltpu.VMEM((192, 256), BF16),
        pltpu.VMEM((7, 32, 256), BF16),
        pltpu.VMEM((NX, 192, 256), BF16),
        pltpu.VMEM((256, 640), BF16),
        pltpu.VMEM((7, 32, 640), BF16),
        pltpu.VMEM((3, 8, 128), F32),
        pltpu.VMEM((7, 8, 128), F32),
        pltpu.VMEM((3, 8, 128), F32),
        pltpu.VMEM((7, 8, 128), F32),
        pltpu.SemaphoreType.DMA((N_SEMS,)),
        pltpu.SemaphoreType.DMA((N_SEMS,)),
        pltpu.SemaphoreType.DMA,
    ]
    exchange, back, scal = pl.pallas_call(
        kernel,
        out_shape=(
            jax.ShapeDtypeStruct((out_rows, rows), F32),
            jax.ShapeDtypeStruct((32, 640), F32),
            jax.ShapeDtypeStruct((8, 128), F32),
        ),
        in_specs=[vmem, vmem, pl.BlockSpec(memory_space=pl.ANY)],
        out_specs=(vmem, vmem, vmem),
        scratch_shapes=scratch,
        compiler_params=pltpu.CompilerParams(
            collective_id=0, has_side_effects=True, vmem_limit_bytes=56 * 1024 * 1024
        ),
        name="admm_exchange",
    )(orbitals, projector, integrals)
    trace_mean = scal[0, 0] / total_adm
    energy_mean = -0.5 * scal[1, 0] / (total_adm * nocc)
    return exchange, back[0 : nocc // NG, 0:npri].T, energy_mean, trace_mean


def solution(mesh):
    return jax.shard_map(
        on_device,
        mesh=mesh,
        in_specs=(P("gx", None), P("gy", "gx"), P("gx", "gy", None)),
        out_specs=(P("gx", "gy"), P("gx", "gy"), P(), P()),
        check_vma=False,
    )
```

time: 447 us -> 135 us (0.30)
  the two profiles are of different devices: /device:TPU:9 before, /device:TPU:17 now
where the time goes in v1:
time: 135 us
  Pallas kernels  124 us (92%)
  local copies, waits for them, and re-layouts  6.56 us (5%)
  between operations  4.2 us (3%)
    pallas_call x1, Pallas kernels, on_device(): pl.pallas_call(kernel, out_shape=(jax.ShapeDtypeStruct((out_rows, rows),...  124 us
    unnamed x2, local copies, waits for them, and re-layouts  3.76 us

profile of v1, /device:TPU:17, one launch (start us, length us, event | category | flops | bytes accessed | tf_op | source)
XLA Modules:
  0.0 134.6 jit_solution(551453063855298687)
XLA Ops:
  0.6 1.8 %copy.7.orb_ref = bf16[625,200]{1,0:T(8,128)(2,1)} copy(bf16[625,200]{0,1:T(8,128)(2,1)} %param.3) | data formatting | bytes 500000 | tf_op args[0]
  2.5 123.9 %admm_exchange.1 = (f32[188,752]{1,0:T(8,128)}, f32[32,640]{1,0:T(8,128)}, f32[8,128]{1,0:T(8,128)}) custom-call(bf16[625,200]{1,0:T(8,128)(2,1)} %copy.7.orb_ref, bf16[752,625]{1,0:T(8,128)(2,1)} %proj_ref.1, bf16[1,752,6016]{2,1,0:T(8,128)(2,1)} %int_ref.1), custom_call_target="tpu_custom_call" | custom-call | tf_op jit(solution)/shard_map/admm_exchange/pallas_call | solution.py:475
  126.4 1.3 fusion
  128.9 1.5 %slice_bitcast_fusion = f32[625,25]{0,1:T(8,128)} fusion(f32[32,640]{1,0:T(8,128)} %get-tuple-element.8), kind=kLoop, calls=%fused_computation | loop fusion | bytes 125000 | tf_op jit(solution)/shard_map/transpose | solution.py:492
  130.5 1.9 %copy.9 = f32[188,752]{1,0:T(8,128)} copy(f32[188,752]{1,0:T(8,128)} %get-tuple-element.16) | data formatting | bytes 1131008

commit v2 on v1

v2 whole, which is shorter than its diff:
```python
import functools

import jax
import jax.numpy as jnp
from jax import lax
from jax.experimental import pallas as pl
from jax.experimental.pallas import tpu as pltpu
from jax.sharding import PartitionSpec as P

MESH = pl.DeviceIdType.MESH
F32, BF16 = jnp.float32, jnp.bfloat16
NZ, NX, NY, NC = 8, 4, 4, 2
NG = NY * NC
PIECES = 6


def dot(a, b, ca, cb):
    return lax.dot_general(a, b, (((ca,), (cb,)), ((), ())), preferred_element_type=F32)


LAG = 3
D_AT = [0,5,9,14,18,22,26,29,34]


class Links:
    def __init__(self, send_sems, recv_sems, partner):
        self.send_sems, self.recv_sems, self.partner = send_sems, recv_sems, partner
        self.n_send = self.n_recv = 0
        self.pending = []

    def slot(self):
        self.n_recv += 1
        return self.n_recv - 1

    def send(self, src, dst, device, slot, pred=None):
        copy = pltpu.make_async_remote_copy(
            src_ref=src,
            dst_ref=dst,
            send_sem=self.send_sems.at[self.n_send],
            recv_sem=self.recv_sems.at[slot],
            device_id=device,
            device_id_type=MESH,
        )
        self.n_send += 1
        self.pending.append((copy, pred))
        if pred is None:
            copy.start()
        else:
            pl.when(pred)(copy.start)

    def arrived(self, dst, slot, pred=None):
        copy = pltpu.make_async_remote_copy(
            src_ref=dst,
            dst_ref=dst,
            send_sem=self.send_sems.at[0],
            recv_sem=self.recv_sems.at[slot],
            device_id=self.partner,
            device_id_type=MESH,
        )
        if pred is None:
            copy.wait_recv()
        else:
            pl.when(pred)(copy.wait_recv)

    def drain(self):
        for copy, pred in self.pending:
            if pred is None:
                copy.wait_send()
            else:
                pl.when(pred)(copy.wait_send)
        self.pending = []


def together(*flows):
    flows = list(flows)
    while flows:
        for flow in list(flows):
            if next(flow, "end") == "end":
                flows.remove(flow)
        yield


def interleave(*flows):
    for _ in together(*flows):
        pass


def kernel(
    orb_ref,
    proj_ref,
    int_ref,
    exch_ref,
    back_ref,
    scal_ref,
    iv,
    pp,
    part,
    xs,
    xr,
    zs,
    zr,
    stage,
    full,
    hf,
    h16,
    hp,
    hh,
    acc,
    psend,
    prcv,
    ts,
    tr,
    tfull,
    dxs,
    dxr,
    dzs,
    dzr,
    ap,
    bk,
    bkr,
    sc,
    sr1,
    sr2,
    sr3,
    send_sems,
    recv_sems,
    int_sem,
):
    gx, gy = lax.axis_index("gx"), lax.axis_index("gy")
    z, x = gx // NX, gx % NX
    y, c = gy // NC, gy % NC
    rows = proj_ref.shape[0]
    npri = proj_ref.shape[1]
    nocc = orb_ref.shape[0]
    out_rows = rows // NX

    load = pltpu.make_async_copy(int_ref.at[0], iv, int_sem)
    load.start()

    def at(dz=0, dx=0, dy=0, dg=0):
        zz, xx = (z + dz) % NZ, (x + dx) % NX
        if dg:
            gg = (gy + dg) % NG
        else:
            gg = ((y + dy) % NY) * NC + c
        return (zz * NX + xx, gg)

    partner = (gx, y * NC + (1 - c))
    links = Links(send_sems, recv_sems, partner)

    barrier = pltpu.get_barrier_semaphore()
    peers = [at(dz=d) for d in range(1, NZ)] + [at(dx=d) for d in range(1, NX)]
    peers += [at(dg=d) for d in range(1, NG)]
    for peer in peers:
        pl.semaphore_signal(barrier, inc=1, device_id=peer, device_id_type=MESH)

    part[...] = jnp.zeros_like(part)
    share = dot(proj_ref[...], orb_ref[...], 1, 1)
    part[0, 0:rows, :] = share[:, 0:128]
    part[1, 0:rows, 0 : nocc - 128] = share[:, 128:nocc]
    pl.semaphore_wait(barrier, len(peers))

    def ring4(dim, part_of, on_arrival=None):
        me = {"x": x, "y": y}[dim]
        step = (lambda d: at(dx=d)) if dim == "x" else (lambda d: at(dy=d))
        left, right, far = (me + 3) % 4, (me + 1) % 4, (me + 2) % 4
        from_left, from_right, from_far = [[links.slot(), links.slot()] for _ in range(3)]

        def send(i, h, d, slots):
            links.send(part_of(i, h), part_of(i, h), step(d), slots[h])

        def arrived(i, h, slots):
            links.arrived(part_of(i, h), slots[h])

        def seen(i, h):
            if on_arrival:
                on_arrival(part_of, i, h)

        send(me, 0, 1, from_left)
        send(me, 1, 3, from_right)
        send(me, 1, 1, from_left)
        send(me, 0, 3, from_right)
        yield
        arrived(left, 0, from_left)
        send(left, 0, 1, from_far)
        arrived(right, 1, from_right)
        send(right, 1, 3, from_far)
        seen(left, 0)
        seen(right, 1)
        yield
        arrived(left, 1, from_left)
        arrived(right, 0, from_right)
        seen(left, 1)
        seen(right, 0)
        for h in range(2):
            arrived(far, h, from_far)
            seen(far, h)

    def direct4(dim, whole):
        me = {"x": x, "y": y}[dim]
        step = (lambda d: at(dx=d)) if dim == "x" else (lambda d: at(dy=d))
        slots = [links.slot() for _ in range(3)]
        for d in (2, 1, 3):
            links.send(whole(me), whole(me), step(d), slots[d - 1])
        yield
        for d in (1, 3, 2):
            links.arrived(whole((me + 4 - d) % 4), slots[d - 1])

    def reduce_xz(src_ref, xs, xr, zs, zr, piece, lanes):
        xs[lanes] = src_ref[lanes].astype(BF16)
        slots = [links.slot() for _ in range(1, NX)]
        for d in (2, 1, 3):
            to = (x + d) % NX
            links.send(xs.at[lanes, pl.ds(to * 192, 192)], xr.at[lanes, d - 1], at(dx=d), slots[d - 1])
        yield
        total = src_ref[lanes, pl.ds(x * 192, 192)]
        for d in (1, 3, 2):
            links.arrived(xr.at[lanes, d - 1], slots[d - 1])
            total = total + xr[lanes, d - 1].astype(F32)
        src_ref[lanes, pl.ds(x * 192, 192)] = total
        zs[lanes] = total.astype(BF16)
        slots = [links.slot() for _ in range(1, NZ)]
        for d in (4, 3, 5, 2, 6, 1, 7):
            to = (z + d) % NZ
            first = jnp.minimum(to, PIECES - 1) * 32
            links.send(zs.at[lanes, pl.ds(first, 32)], zr.at[lanes, d - 1], at(dz=d), slots[d - 1], to < PIECES)
        yield
        owner = z < PIECES
        for d in range(1, NZ):
            links.arrived(zr.at[lanes, d - 1], slots[d - 1], owner)

        own = jnp.minimum(z, PIECES - 1)

        @pl.when(owner)
        def _():
            total = src_ref[lanes, pl.ds(x * 192 + own * 32, 32)]
            for d in range(1, NZ):
                total = total + zr[lanes, d - 1].astype(F32)
            piece(x, own)[...] = total.astype(BF16)

        slots = [links.slot() for _ in range(1, NZ)]
        for d in (4, 3, 5, 2, 6, 1, 7):
            links.send(piece(x, own), piece(x, own), at(dz=d), slots[d - 1], owner)
        yield
        for d in range(1, NZ):
            src = (z + NZ - d) % NZ
            links.arrived(piece(x, jnp.minimum(src, PIECES - 1)), slots[d - 1], src < PIECES)

    def flow_admm(lanes):
        waits = []

        def to_partner(other):
            def go(part_of, i, h):
                slot = links.slot()
                links.send(part_of(i, h), part_of(i, h), partner, slot)
                waits.append((other, i, h, slot))

            return go

        yield from reduce_xz(part, xs, xr, zs, zr, lambda i, k: stage.at[lanes, y, c, i, pl.ds(k * 32, 32)], lanes)
        yield from together(
            direct4("x", lambda i: stage.at[lanes, y, c, i, 0:96]),
            direct4("y", lambda i: stage.at[lanes, i, c, x, 96:192]),
        )
        low = lambda i, h: stage.at[lanes, i, c, 2 * h : 2 * h + 2, 0:96]
        high = lambda i, h: stage.at[lanes, 2 * h : 2 * h + 2, c, i, 96:192]
        low_sent = to_partner(lambda i, h: stage.at[lanes, i, 1 - c, 2 * h : 2 * h + 2, 0:96])
        high_sent = to_partner(lambda i, h: stage.at[lanes, 2 * h : 2 * h + 2, 1 - c, i, 96:192])
        both = together(ring4("y", low, low_sent), ring4("x", high, high_sent))
        next(both)
        for h in range(2):
            low_sent(low, y, h)
            high_sent(high, x, h)
        yield
        yield from both
        for other, i, h, slot in waits:
            links.arrived(other(i, h), slot)

    def housekeeping():
        pp[...] = jnp.zeros_like(pp)
        pp[0:rows, 0:npri] = proj_ref[...]
        hf[...] = jnp.zeros_like(hf)
        hp[...] = jnp.zeros_like(hp)
        yield

    flows = [flow_admm(0), flow_admm(1)]
    interleave(*flows, housekeeping())
    for a in range(NY):
        for b in range(NC):
            for k in range(NX):
                n = min(192, rows - 192 * k)
                r0 = rows * (a * NC + b) + 192 * k
                full[r0 : r0 + n, 0:128] = stage[0, a, b, k, 0:n, :]
                full[r0 : r0 + n, 128:256] = stage[1, a, b, k, 0:n, :]

    load.wait()
    for r0 in range(0, rows, 256):
        n = min(256, rows - r0)
        hf[r0 : r0 + n, :] = dot(iv[r0 : r0 + n, :], full[...], 1, 0)
    h16[...] = hf[...].astype(BF16)
    hr = h16[...].astype(F32)
    trace = jnp.sum(hr * hr)
    for k in range(NX):
        hp[192 * k : 192 * k + out_rows, :] = hf[out_rows * k : out_rows * (k + 1), :]
    ht = jnp.transpose(hp[...])[0:208, :].astype(BF16)
    for j in range(6):
        hh[0, 0, j] = ht[:, 128 * j : 128 * j + 128]

    ys, cs = z // NC, z % NC
    dy = (y + NY - ys) % NY
    on = c == cs
    is_src = on & (dy == 0)
    lhs_at = jnp.where(is_src, 0, 1)
    up, down, yup, ydown = at(dz=1), at(dz=NZ - 1), at(dy=1), at(dy=NY - 1)

    def piece_of(which, s, j):
        return hh.at[which, s, j]

    def accumulate(s, first=False):
        @pl.loop(0, 6)
        def _(m):
            cols = pl.ds(pl.multiple_of(m * 128, 128), 128)
            value = dot(hh[lhs_at, s, m], jnp.concatenate([hh[0, s, j] for j in range(6)], 1), 0, 0)
            if first:
                acc[cols, :] = value
            else:
                acc[cols, :] += value

    def flow_exchange():
        col_slots = {(s, j): links.slot() for s in range(1, NZ) for j in range(6)}
        row_slots = {(s, j): links.slot() for s in range(NZ) for j in range(6)}
        pairs = {e - 2: [(0, e), (0, 5 - e)] for e in range(3)}
        for k in (1, 2, 3):
            for j in range(6):
                pairs[6 * k - 5 + j] = [(k, j), (8 - k, 5 - j)]
        for j in range(3):
            pairs[19 + j] = [(4, j), (4, 5 - j)]

        def pass_on(s, j):
            if s in (0, 1, 2) or (s == 3 and j < 3):
                links.send(piece_of(0, s, j), piece_of(0, s + 1, j), up, col_slots[s + 1, j])
            if s in (0, 7, 6) or (s == 5 and j >= 3):
                t = (s - 1) % 8
                links.send(piece_of(0, s, j), piece_of(0, t, j), down, col_slots[t, j])

        def spread(s, j):
            src, dst = piece_of(0, s, j), piece_of(1, s, j)
            links.send(src, dst, yup if j < 3 else ydown, row_slots[s, j], is_src)
            links.send(src, dst, partner, row_slots[s, j], is_src)

        def relay(s, j, h):
            blk = piece_of(1, s, j)
            here = on & (dy == (h if j < 3 else 4 - h))
            links.arrived(blk, row_slots[s, j], here)
            if h < 3:
                links.send(blk, blk, yup if j < 3 else ydown, row_slots[s, j], here)
            links.send(blk, blk, partner, row_slots[s, j], here)

        def finish_slot(s):
            for j in range(6):
                links.arrived(piece_of(1, s, j), row_slots[s, j], jnp.logical_not(on))
            accumulate(s, s == 0)

        for j in range(6):
            pass_on(0, [0, 5, 1, 4, 2, 3][j])
        yield
        for j in range(6):
            spread(0, [0, 5, 1, 4, 2, 3][j])
        yield
        last = 21 + 3 * LAG
        for e in range(0, last + 1):
            if 1 <= e <= 21:
                for s, j in pairs[e]:
                    links.arrived(piece_of(0, s, j), col_slots[s, j])
                    pass_on(s, j)
                    spread(s, j)
            for h in (1, 2, 3):
                for s, j in pairs.get(e - LAG * h, ()):
                    relay(s, j, h)
            q = e - 3 * LAG - 1
            if q == 0:
                finish_slot(0)
            elif q in (6, 12, 18):
                finish_slot(q // 6)
                finish_slot(8 - q // 6)
            yield
        finish_slot(4)
        slots = [links.slot() for _ in range(6)]
        left, right, far = (x + 3) % NX, (x + 1) % NX, (x + 2) % NX
        to_right, to_left = at(dx=1), at(dx=3)
        def mine(i, h):
            return acc[pl.ds(i * 192, 192), 384 * h : 384 * h + 384]

        psend[0] = mine(far, 0).astype(BF16)
        links.send(psend.at[0], prcv.at[0], to_right, slots[0])
        psend[1] = mine(far, 1).astype(BF16)
        links.send(psend.at[1], prcv.at[1], to_left, slots[1])
        psend[2] = mine(right, 1).astype(BF16)
        links.send(psend.at[2], prcv.at[2], to_right, slots[2])
        psend[3] = mine(left, 0).astype(BF16)
        links.send(psend.at[3], prcv.at[3], to_left, slots[3])
        yield
        links.arrived(prcv.at[0], slots[0])
        psend[4] = (mine(right, 0) + prcv[0].astype(F32)).astype(BF16)
        links.send(psend.at[4], prcv.at[4], to_right, slots[4])
        links.arrived(prcv.at[1], slots[1])
        psend[5] = (mine(left, 1) + prcv[1].astype(F32)).astype(BF16)
        links.send(psend.at[5], prcv.at[5], to_left, slots[5])
        yield
        for j in (2, 3, 4, 5):
            links.arrived(prcv.at[j], slots[j])
        first = mine(x, 0) + prcv[3].astype(F32) + prcv[4].astype(F32)
        second = mine(x, 1) + prcv[2].astype(F32) + prcv[5].astype(F32)
        total = jnp.concatenate([first, second], 1)
        lane = lax.broadcasted_iota(jnp.int32, total.shape, 1)
        out = total
        for k in range(1, NX):
            moved = pltpu.roll(total, total.shape[1] - 4 * k, 1)
            out = jnp.where(lane >= out_rows * k, moved, out)
        exch_ref[...] = out[0:out_rows, 0:rows]

    def flow_applied():
        own = jnp.concatenate([stage[i, y, c].reshape(4 * 192, 128) for i in range(2)], 1)
        tt = dot(own, h16[...], 0, 0).astype(BF16)
        share = nocc // NG
        r = lax.broadcasted_iota(jnp.int32, (256, 256), 0)
        j = lax.broadcasted_iota(jnp.int32, (256, 256), 1)
        pick = ((r % 32 < share) & (j == share * (r // 32) + r % 32)).astype(F32).astype(BF16)
        ts[...] = dot(pick, tt, 1, 0).astype(BF16)
        slots = [links.slot() for _ in range(1, NG)]
        for d in range(1, NG):
            to = (gy + d) % NG
            links.send(ts.at[pl.ds(to * 32, 32), :], tr.at[d - 1], at(dg=d), slots[d - 1])
        yield
        total = ts[pl.ds(gy * 32, 32), :].astype(F32)
        for d in range(1, NG):
            links.arrived(tr.at[d - 1], slots[d - 1])
            total = total + tr[d - 1].astype(F32)
        energy = jnp.sum(total * total)
        tfull[pl.ds(gy * 32, 32), :] = total.astype(BF16)
        slots = [links.slot() for _ in range(1, NG)]
        s1 = [links.slot() for _ in range(1, NG)]
        mine = tfull.at[pl.ds(gy * 32, 32), :]
        sc[0] = jnp.where(lax.broadcasted_iota(jnp.int32, (8, 128), 0) == 0, trace, energy)
        for d in range(1, NG):
            links.send(mine, mine, at(dg=d), slots[d - 1])
            links.send(sc.at[0], sr1.at[d - 1], at(dg=d), s1[d - 1])
        yield
        for d in range(1, NG):
            src = (gy + NG - d) % NG
            links.arrived(tfull.at[pl.ds(src * 32, 32), :], slots[d - 1])
        applied = dot(h16[...], tfull[...], 1, 1)
        part[0] = applied[:, 0:128]
        part[1] = applied[:, 128:256]
        total = sc[0]
        for d in range(1, NG):
            links.arrived(sr1.at[d - 1], s1[d - 1])
            total = total + sr1[d - 1]
        sc[1] = total
        s2 = [links.slot() for _ in range(1, NX)]
        for d in range(1, NX):
            links.send(sc.at[1], sr2.at[d - 1], at(dx=d), s2[d - 1])
        for _ in reduce_xz(part, dxs, dxr, dzs, dzr, lambda i, k: ap.at[:, i, pl.ds(k * 32, 32)], slice(0, 2)):
            yield
        total = sc[1]
        for d in range(1, NX):
            links.arrived(sr2.at[d - 1], s2[d - 1])
            total = total + sr2[d - 1]
        sc[2] = total
        s3 = [links.slot() for _ in range(1, NZ)]
        for d in range(1, NZ):
            links.send(sc.at[2], sr3.at[d - 1], at(dz=d), s3[d - 1])
        for _ in ring4("x", lambda i, h: ap.at[h, i]):
            yield
        whole = jnp.concatenate([ap[i].reshape(4 * 192, 128) for i in range(2)], 1)
        bt = dot(whole, pp[...], 0, 0)
        bk[...] = bt.astype(BF16)
        slots = [links.slot() for _ in range(1, NG)]
        for d in range(1, NG):
            to = (gy + d) % NG
            links.send(bk.at[pl.ds(to * 32, 32), :], bkr.at[d - 1], at(dg=d), slots[d - 1])
        yield
        total = bk[pl.ds(gy * 32, 32), :].astype(F32)
        for d in range(1, NG):
            links.arrived(bkr.at[d - 1], slots[d - 1])
            total = total + bkr[d - 1].astype(F32)
        back_ref[...] = total
        total = sc[2]
        for d in range(1, NZ):
            links.arrived(sr3.at[d - 1], s3[d - 1])
            total = total + sr3[d - 1]
        scal_ref[...] = total

    exchange, applied = flow_exchange(), flow_applied()
    for step, _ in enumerate(exchange):
        for _ in range(D_AT.count(step)):
            next(applied, None)
    for _ in applied:
        pass
    links.drain()


N_SEMS = 720


def finish(total_adm, nocc, exch_ref, back_ref, scal_ref, exch_out, back_out, energy_out, trace_out):
    exch_out[...] = exch_ref[...]
    back_out[...] = back_ref[0 : back_out.shape[0], 0 : back_out.shape[1]]
    trace_out[...] = scal_ref[0:1, 0:1] / total_adm
    energy_out[...] = -0.5 * scal_ref[1:2, 0:1] / (total_adm * nocc)


def on_device(orbitals, projector, integrals):
    rows, npri = projector.shape
    total_adm = integrals.shape[2]
    nocc = orbitals.shape[1]
    out_rows = rows // NX
    vmem = pl.BlockSpec(memory_space=pltpu.VMEM)
    scratch = [
        pltpu.VMEM((rows, total_adm), BF16),
        pltpu.VMEM((768, 640), BF16),
        pltpu.VMEM((2, 768, 128), F32),
        pltpu.VMEM((2, 768, 128), BF16),
        pltpu.VMEM((2, 3, 192, 128), BF16),
        pltpu.VMEM((2, 192, 128), BF16),
        pltpu.VMEM((2, 7, 32, 128), BF16),
        pltpu.VMEM((2, NY, NC, NX, 192, 128), BF16),
        pltpu.VMEM((total_adm, 256), BF16),
        pltpu.VMEM((768, 256), F32),
        pltpu.VMEM((768, 256), BF16),
        pltpu.VMEM((768, 256), F32),
        pltpu.VMEM((2, NZ, 6, 208, 128), BF16),
        pltpu.VMEM((768, 768), F32),
        pltpu.VMEM((6, 192, 384), BF16),
        pltpu.VMEM((6, 192, 384), BF16),
        pltpu.VMEM((256, 256), BF16),
        pltpu.VMEM((7, 32, 256), BF16),
        pltpu.VMEM((256, 256), BF16),
        pltpu.VMEM((2, 768, 128), BF16),
        pltpu.VMEM((2, 3, 192, 128), BF16),
        pltpu.VMEM((2, 192, 128), BF16),
        pltpu.VMEM((2, 7, 32, 128), BF16),
        pltpu.VMEM((2, NX, 192, 128), BF16),
        pltpu.VMEM((256, 640), BF16),
        pltpu.VMEM((7, 32, 640), BF16),
        pltpu.VMEM((3, 8, 128), F32),
        pltpu.VMEM((7, 8, 128), F32),
        pltpu.VMEM((3, 8, 128), F32),
        pltpu.VMEM((7, 8, 128), F32),
        pltpu.SemaphoreType.DMA((N_SEMS,)),
        pltpu.SemaphoreType.DMA((N_SEMS,)),
        pltpu.SemaphoreType.DMA,
    ]
    exchange, back, scal = pl.pallas_call(
        kernel,
        out_shape=(
            jax.ShapeDtypeStruct((out_rows, rows), F32),
            jax.ShapeDtypeStruct((32, 640), F32),
            jax.ShapeDtypeStruct((8, 128), F32),
        ),
        in_specs=[vmem, vmem, pl.BlockSpec(memory_space=pl.ANY)],
        out_specs=(vmem, vmem, vmem),
        scratch_shapes=scratch,
        compiler_params=pltpu.CompilerParams(
            collective_id=0, has_side_effects=True, vmem_limit_bytes=56 * 1024 * 1024
        ),
        name="admm_exchange",
    )(orbitals.T, projector, integrals)
    exchange, back, energy_mean, trace_mean = pl.pallas_call(
        functools.partial(finish, total_adm, nocc),
        out_shape=(
            jax.ShapeDtypeStruct((out_rows, rows), F32),
            jax.ShapeDtypeStruct((nocc // NG, npri), F32),
            jax.ShapeDtypeStruct((1, 1), F32),
            jax.ShapeDtypeStruct((1, 1), F32),
        ),
        in_specs=[vmem] * 3,
        out_specs=(vmem,) * 4,
        name="finish",
    )(exchange, back, scal)
    return exchange, back.T, energy_mean.reshape(()), trace_mean.reshape(())


def solution(mesh):
    return jax.shard_map(
        on_device,
        mesh=mesh,
        in_specs=(P("gx", None), P("gy", "gx"), P("gx", "gy", None)),
        out_specs=(P("gx", "gy"), P("gx", "gy"), P(), P()),
        check_vma=False,
    )
```

time: 135 us -> 118 us (0.87)
  the two profiles are of different devices: /device:TPU:17 before, /device:TPU:9 now
where the time goes in v2:
time: 118 us
  Pallas kernels  117 us (99%)
    pallas_call x1, Pallas kernels, on_device(): pl.pallas_call(kernel, out_shape=(jax.ShapeDtypeStruct((out_rows, rows),...  115 us

profile of v2, /device:TPU:9, one launch (start us, length us, event | category | flops | bytes accessed | tf_op | source)
XLA Modules:
  0.0 117.6 jit_solution(11697165536065772692)
XLA Ops:
  0.6 114.9 %admm_exchange.1 = (f32[188,752]{1,0:T(8,128)}, f32[32,640]{1,0:T(8,128)}, f32[8,128]{1,0:T(8,128)}) custom-call(bf16[200,625]{1,0:T(8,128)(2,1)} %bitcast.4, bf16[752,625]{1,0:T(8,128)(2,1)} %proj_ref.1, bf16[1,752,6016]{2,1,0:T(8,128)(2,1)} %int_ref.1), custom_call_target="tpu_custom_call" | custom-call | tf_op jit(solution)/shard_map/admm_exchange/pallas_call | solution.py:554
  115.6 2.0 %finish.1 = (f32[188,752]{1,0:T(8,128)}, f32[25,625]{1,0:T(8,128)}, f32[1,1]{1,0:T(1,128)}, f32[1,1]{1,0:T(1,128)}) custom-call(f32[188,752]{1,0:T(8,128)} %get-tuple-element.11.exch_ref, f32[32,640]{1,0:T(8,128)} %get-tuple-element.12.back_ref, f32[8,128]{1,0:T(8,128)} %get-tuple-element.13.scal_ref), custom_call_target="tpu_custom_call" | custom-call | tf_op jit(solution)/shard_map/finish/pallas_call | solution.py:569

commit v3 on v2

--- a/solution.py
+++ b/solution.py
@@ -19,7 +19,7 @@
 
 
 LAG = 3
-D_AT = [0,5,9,14,18,22,26,29,34]
+D_AT = [1,7,13,19,25,30,32,33,34]
 
 
 class Links:
@@ -86,12 +86,14 @@
 
 
 def kernel(
-    orb_ref,
-    proj_ref,
+    orb_hbm,
+    proj_hbm,
     int_ref,
     exch_ref,
     back_ref,
     scal_ref,
+    orb_ref,
+    proj_ref,
     iv,
     pp,
     part,
@@ -134,8 +136,9 @@
     nocc = orb_ref.shape[0]
     out_rows = rows // NX
 
-    load = pltpu.make_async_copy(int_ref.at[0], iv, int_sem)
-    load.start()
+    load = pltpu.make_async_copy(int_ref.at[0], iv, int_sem.at[0])
+    load_proj = pltpu.make_async_copy(proj_hbm, proj_ref, int_sem.at[1])
+    load_orb = pltpu.make_async_copy(orb_hbm, orb_ref, int_sem.at[2])
 
     def at(dz=0, dx=0, dy=0, dg=0):
         zz, xx = (z + dz) % NZ, (x + dx) % NX
@@ -153,8 +156,13 @@
     peers += [at(dg=d) for d in range(1, NG)]
     for peer in peers:
         pl.semaphore_signal(barrier, inc=1, device_id=peer, device_id_type=MESH)
+    load_orb.start()
+    load_proj.start()
+    load.start()
 
     part[...] = jnp.zeros_like(part)
+    load_orb.wait()
+    load_proj.wait()
     share = dot(proj_ref[...], orb_ref[...], 1, 1)
     part[0, 0:rows, :] = share[:, 0:128]
     part[1, 0:rows, 0 : nocc - 128] = share[:, 128:nocc]
@@ -316,15 +324,22 @@
     def piece_of(which, s, j):
         return hh.at[which, s, j]
 
-    def accumulate(s, first=False):
-        @pl.loop(0, 6)
+    def accumulate_half(slots, m, first=False):
+        lhs = jnp.concatenate(
+            [jnp.concatenate([hh[lhs_at, s, 3 * m + i] for i in range(3)], 1) for s in slots], 0
+        )
+        rhs = jnp.concatenate([jnp.concatenate([hh[0, s, j] for j in range(6)], 1) for s in slots], 0)
+        value = dot(lhs, rhs, 0, 0)
+        here = pl.ds(pl.multiple_of(m * 384, 384), 384)
+        if first:
+            acc[here, :] = value
+        else:
+            acc[here, :] += value
+
+    def accumulate(*slots, first=False):
+        @pl.loop(0, 2)
         def _(m):
-            cols = pl.ds(pl.multiple_of(m * 128, 128), 128)
-            value = dot(hh[lhs_at, s, m], jnp.concatenate([hh[0, s, j] for j in range(6)], 1), 0, 0)
-            if first:
-                acc[cols, :] = value
-            else:
-                acc[cols, :] += value
+            accumulate_half(slots, m, first)
 
     def flow_exchange():
         col_slots = {(s, j): links.slot() for s in range(1, NZ) for j in range(6)}
@@ -356,10 +371,10 @@
                 links.send(blk, blk, yup if j < 3 else ydown, row_slots[s, j], here)
             links.send(blk, blk, partner, row_slots[s, j], here)
 
-        def finish_slot(s):
-            for j in range(6):
-                links.arrived(piece_of(1, s, j), row_slots[s, j], jnp.logical_not(on))
-            accumulate(s, s == 0)
+        def rows_here(*slots):
+            for s in slots:
+                for j in range(6):
+                    links.arrived(piece_of(1, s, j), row_slots[s, j], jnp.logical_not(on))
 
         for j in range(6):
             pass_on(0, [0, 5, 1, 4, 2, 3][j])
@@ -378,23 +393,26 @@
                 for s, j in pairs.get(e - LAG * h, ()):
                     relay(s, j, h)
             q = e - 3 * LAG - 1
-            if q == 0:
-                finish_slot(0)
-            elif q in (6, 12, 18):
-                finish_slot(q // 6)
-                finish_slot(8 - q // 6)
+            if q in (6, 12, 18):
+                k = q // 6
+                slots = (0, 1, 7) if k == 1 else (k, 8 - k)
+                rows_here(*slots)
+                accumulate(*slots, first=k == 1)
             yield
-        finish_slot(4)
+        rows_here(4)
         slots = [links.slot() for _ in range(6)]
         left, right, far = (x + 3) % NX, (x + 1) % NX, (x + 2) % NX
         to_right, to_left = at(dx=1), at(dx=3)
         def mine(i, h):
             return acc[pl.ds(i * 192, 192), 384 * h : 384 * h + 384]
 
+        far_half = 1 - x // 2
+        accumulate_half((4,), far_half)
         psend[0] = mine(far, 0).astype(BF16)
         links.send(psend.at[0], prcv.at[0], to_right, slots[0])
         psend[1] = mine(far, 1).astype(BF16)
         links.send(psend.at[1], prcv.at[1], to_left, slots[1])
+        accumulate_half((4,), 1 - far_half)
         psend[2] = mine(right, 1).astype(BF16)
         links.send(psend.at[2], prcv.at[2], to_right, slots[2])
         psend[3] = mine(left, 0).astype(BF16)
@@ -517,6 +535,8 @@
     out_rows = rows // NX
     vmem = pl.BlockSpec(memory_space=pltpu.VMEM)
     scratch = [
+        pltpu.VMEM((nocc, npri), BF16),
+        pltpu.VMEM((rows, npri), BF16),
         pltpu.VMEM((rows, total_adm), BF16),
         pltpu.VMEM((768, 640), BF16),
         pltpu.VMEM((2, 768, 128), F32),
@@ -549,7 +569,7 @@
         pltpu.VMEM((7, 8, 128), F32),
         pltpu.SemaphoreType.DMA((N_SEMS,)),
         pltpu.SemaphoreType.DMA((N_SEMS,)),
-        pltpu.SemaphoreType.DMA,
+        pltpu.SemaphoreType.DMA((3,)),
     ]
     exchange, back, scal = pl.pallas_call(
         kernel,
@@ -558,7 +578,7 @@
             jax.ShapeDtypeStruct((32, 640), F32),
             jax.ShapeDtypeStruct((8, 128), F32),
         ),
-        in_specs=[vmem, vmem, pl.BlockSpec(memory_space=pl.ANY)],
+        in_specs=[pl.BlockSpec(memory_space=pl.ANY)] * 3,
         out_specs=(vmem, vmem, vmem),
         scratch_shapes=scratch,
         compiler_params=pltpu.CompilerParams(

time: 118 us -> 110 us (0.932); the launches traced: 118 us -> 108 us
  Pallas kernels: 117 us -> 108 us
    pallas_call x1, Pallas kernels: 115 us -> 106 us  [on_device(): pl.pallas_call(kernel, out_shape=(jax.ShapeDtypeStruct((out_rows, rows),...]
where the time goes in v3:
time: 110 us; the launch traced here: 108 us
  Pallas kernels  108 us (98%)
    pallas_call x1, Pallas kernels, on_device(): pl.pallas_call(kernel, out_shape=(jax.ShapeDtypeStruct((out_rows, rows),...  106 us

profile of v3, /device:TPU:9, one launch (start us, length us, event | category | flops | bytes accessed | tf_op | source)
XLA Modules:
  0.0 108.2 jit_solution(10580711533963540761)
XLA Ops:
  0.6 105.6 %admm_exchange.1 = (f32[188,752]{1,0:T(8,128)}, f32[32,640]{1,0:T(8,128)}, f32[8,128]{1,0:T(8,128)}) custom-call(bf16[200,625]{1,0:T(8,128)(2,1)} %bitcast.4, bf16[752,625]{1,0:T(8,128)(2,1)} %proj_hbm.1, bf16[1,752,6016]{2,1,0:T(8,128)(2,1)} %int_ref.1), custom_call_target="tpu_custom_call" | custom-call | tf_op jit(solution)/shard_map/admm_exchange/pallas_call | solution.py:574
  106.3 2.0 %finish.1 = (f32[188,752]{1,0:T(8,128)}, f32[25,625]{1,0:T(8,128)}, f32[1,1]{1,0:T(1,128)}, f32[1,1]{1,0:T(1,128)}) custom-call(f32[188,752]{1,0:T(8,128)} %get-tuple-element.11.exch_ref, f32[32,640]{1,0:T(8,128)} %get-tuple-element.12.back_ref, f32[8,128]{1,0:T(8,128)} %get-tuple-element.13.scal_ref), custom_call_target="tpu_custom_call" | custom-call | tf_op jit(solution)/shard_map/finish/pallas_call | solution.py:589

commit v4 on v3

--- a/solution.py
+++ b/solution.py
@@ -19,7 +19,7 @@
 
 
 LAG = 3
-D_AT = [1,7,13,19,25,30,32,33,34]
+D_AT = [1,7,13,19,25,30,33,34]
 
 
 class Links:
@@ -358,17 +358,29 @@
                 t = (s - 1) % 8
                 links.send(piece_of(0, s, j), piece_of(0, t, j), down, col_slots[t, j])
 
+        def goes_up(s, j):
+            return j < 3
+
         def spread(s, j):
             src, dst = piece_of(0, s, j), piece_of(1, s, j)
-            links.send(src, dst, yup if j < 3 else ydown, row_slots[s, j], is_src)
+            if s == 4 or goes_up(s, j):
+                links.send(src, dst, yup, row_slots[s, j], is_src)
+            if s == 4 or not goes_up(s, j):
+                links.send(src, dst, ydown, row_slots[s, j], is_src)
             links.send(src, dst, partner, row_slots[s, j], is_src)
 
         def relay(s, j, h):
             blk = piece_of(1, s, j)
-            here = on & (dy == (h if j < 3 else 4 - h))
+            side = h if goes_up(s, j) else 4 - h
+            here = on & (dy == side)
+            if s == 4:
+                if h == 3:
+                    return
+                if h == 1:
+                    here = on & ((dy == 1) | (dy == 3))
             links.arrived(blk, row_slots[s, j], here)
-            if h < 3:
-                links.send(blk, blk, yup if j < 3 else ydown, row_slots[s, j], here)
+            if h < (2 if s == 4 else 3):
+                links.send(blk, blk, yup if goes_up(s, j) else ydown, row_slots[s, j], on & (dy == side))
             links.send(blk, blk, partner, row_slots[s, j], here)
 
         def rows_here(*slots):
@@ -488,7 +500,7 @@
         s3 = [links.slot() for _ in range(1, NZ)]
         for d in range(1, NZ):
             links.send(sc.at[2], sr3.at[d - 1], at(dz=d), s3[d - 1])
-        for _ in ring4("x", lambda i, h: ap.at[h, i]):
+        for _ in direct4("x", lambda i: ap.at[:, i]):
             yield
         whole = jnp.concatenate([ap[i].reshape(4 * 192, 128) for i in range(2)], 1)
         bt = dot(whole, pp[...], 0, 0)

time: 110 us -> 110 us (level); the launches traced: 108 us -> 109 us
    pallas_call x1, Pallas kernels: 106 us -> 107 us  [on_device(): pl.pallas_call(kernel, out_shape=(jax.ShapeDtypeStruct((out_rows, rows),...]
where the time goes in v4:
time: 110 us; the launch traced here: 109 us
  Pallas kernels  109 us (99%)
    pallas_call x1, Pallas kernels, on_device(): pl.pallas_call(kernel, out_shape=(jax.ShapeDtypeStruct((out_rows, rows),...  107 us

profile of v4, /device:TPU:9, one launch (start us, length us, event | category | flops | bytes accessed | tf_op | source)
XLA Modules:
  0.0 109.4 jit_solution(771946698841733513)
XLA Ops:
  0.6 106.8 %admm_exchange.1 = (f32[188,752]{1,0:T(8,128)}, f32[32,640]{1,0:T(8,128)}, f32[8,128]{1,0:T(8,128)}) custom-call(bf16[200,625]{1,0:T(8,128)(2,1)} %bitcast.4, bf16[752,625]{1,0:T(8,128)(2,1)} %proj_hbm.1, bf16[1,752,6016]{2,1,0:T(8,128)(2,1)} %int_ref.1), custom_call_target="tpu_custom_call" | custom-call | tf_op jit(solution)/shard_map/admm_exchange/pallas_call | solution.py:586
  107.5 2.0 %finish.1 = (f32[188,752]{1,0:T(8,128)}, f32[25,625]{1,0:T(8,128)}, f32[1,1]{1,0:T(1,128)}, f32[1,1]{1,0:T(1,128)}) custom-call(f32[188,752]{1,0:T(8,128)} %get-tuple-element.11.exch_ref, f32[32,640]{1,0:T(8,128)} %get-tuple-element.12.back_ref, f32[8,128]{1,0:T(8,128)} %get-tuple-element.13.scal_ref), custom_call_target="tpu_custom_call" | custom-call | tf_op jit(solution)/shard_map/finish/pallas_call | solution.py:601
